TPU v7x, 256 devices: a whole 4x4x8 slice. The times are simulated.
256 devices in a mesh: seq: 64 (over x, z, core), tp: 4 (over y).
Axes of the slice: x: 4, y: 4, z: 8, core: 2. Of those that a mesh axis runs over, the one named last changes fastest.
Arguments:
- layer_in: bfloat16 [49152, 2048], P('seq', 'tp'), may hold values from -6 to 6
- attn_gain: float32 [2048], replicated, may hold values from 0.1 to 1.9
- qkv_weight: bfloat16 [3, 2048, 1024], P(None, None, 'tp'), may hold values from -0.125 to 0.125
- log_decay: float32 [8, 49152], P('tp', 'seq'), may hold values from -0.1 to 0
- write_rate: float32 [8, 49152], P('tp', 'seq'), may hold values from 0 to 0.9
- head_gain: float32 [128], replicated, may hold values from 0.1 to 1.9
- out_weight: bfloat16 [1024, 2048], P('tp'), may hold values from -0.1875 to 0.1875
- ffn_gain: float32 [2048], replicated, may hold values from 0.1 to 1.9
- gate_weight: bfloat16 [2048, 2560], P(None, 'tp'), may hold values from -0.125 to 0.125
- up_weight: bfloat16 [2048, 2560], P(None, 'tp'), may hold values from -0.125 to 0.125
- down_weight: bfloat16 [2560, 2048], P('tp'), may hold values from -0.125 to 0.125
Outputs:
- layer_out: bfloat16 [49152, 2048], P('seq', 'tp')
All inputs are finite; a program needn't handle non-finite values.
Results may differ from a plain program's by a relative error of at most 0.014.
Values may be sent and summed in bfloat16 or wider, within the bound.
A program may use at most 128 MiB of HBM per device.

v0:
```python
import jax
import jax.numpy as jnp
from jax import lax
from jax.sharding import Mesh
from jax.sharding import PartitionSpec as P

SEQ = ("seq_0", "seq_1", "seq_2")
norm_floor = 0.1
head_floor = 0.05
highest = lax.Precision.HIGHEST


def nothing_yet(shard, identity):
    return jax.tree.map(
        lambda a, e: jnp.broadcast_to(jnp.asarray(e, a.dtype), a.shape), shard, identity
    )


def prefix_by_axis(shard, axes, combine, identity):
    before = start = nothing_yet(shard, identity)
    subtotal = shard
    for axis in reversed(axes):
        peers, here = (lax.axis_size(axis), lax.axis_index(axis))
        pieces = jax.tree.map(
            lambda part, kind: lax.all_gather(part.astype(kind), axis),
            subtotal,
            jax.tree.map(lambda a: jnp.bfloat16 if a.dtype == jnp.float32 else a.dtype, shard),
        )
        inside, subtotal = (start, start)
        for k in range(peers):
            passed = k < here
            subtotal = combine(
                subtotal, jax.tree.map(lambda part, own: part[k].astype(own.dtype), pieces, shard)
            )
            inside = jax.tree.map(lambda new, old: jnp.where(passed, new, old), subtotal, inside)
        before = combine(inside, before)
    return before


def in_blocks(shard, dim, peers):
    before, after = (shard.shape[:dim], shard.shape[dim + 1 :])
    return jnp.moveaxis(shard.reshape(*before, peers, -1, *after), dim, 0)


def summed_on_arrival(shard, axis, dim):
    peers = lax.axis_size(axis)
    pieces = lax.all_to_all(in_blocks(shard, dim, peers), axis, 0, 0, tiled=True)
    return jnp.sum(pieces.astype(jnp.float32), axis=0)


def from_everyone(shard, axis):
    peers = lax.axis_size(axis)
    return lax.all_to_all(
        jnp.broadcast_to(shard[None], (peers, *shard.shape)), axis, 0, 0, tiled=True
    )


def of_everyone(shard, axis):
    everything = from_everyone(shard, axis)
    return jnp.sum(everything, axis=0)


def unit_rows(vectors):
    return vectors * lax.rsqrt(jnp.sum(vectors * vectors, axis=-1, keepdims=True) + 1.0)


def compose(earlier, later):
    first_map, first_shift = earlier
    second_map, second_shift = later
    joined_map = jnp.einsum("hij,hjk->hik", second_map, first_map, precision=highest)
    joined_shift = (
        jnp.einsum("hij,hjk->hik", second_map, first_shift, precision=highest) + second_shift
    )
    return (joined_map, joined_shift)


def block_terms(queries, key_rows, values, log_decay, write_rate):
    length = key_rows.shape[2]
    width = key_rows.shape[3]
    cumul = jnp.cumsum(log_decay, axis=2)
    spread = cumul[:, :, :, None] - cumul[:, :, None, :]
    row_ids = lax.broadcasted_iota(jnp.int32, (length, length), 0)
    col_ids = lax.broadcasted_iota(jnp.int32, (length, length), 1)
    inclusive = row_ids >= col_ids
    strict = row_ids > col_ids
    weight_decay = jnp.where(inclusive, jnp.exp(jnp.minimum(spread, 0.0)), 0.0)
    key_key = jnp.einsum("hcte,hcse->hcts", key_rows, key_rows, precision=highest)
    query_key = jnp.einsum("hcte,hcse->hcts", queries, key_rows, precision=highest)
    lower_part = jnp.where(strict, write_rate[:, :, :, None] * key_key * weight_decay, 0.0)
    system = lower_part + jnp.eye(length, dtype=jnp.float32)
    growth = jnp.exp(cumul)
    right_side = jnp.concatenate(
        [write_rate[:, :, :, None] * values, (write_rate * growth)[:, :, :, None] * key_rows],
        axis=3,
    )
    solved = jax.scipy.linalg.solve_triangular(system, right_side, lower=True, unit_diagonal=True)
    wy_value = solved[:, :, :, :width]
    wy_key = solved[:, :, :, width:]
    mixing = query_key * weight_decay
    keys_tail = key_rows * jnp.exp(cumul[:, :, -1:] - cumul)[:, :, :, None]
    transfer = growth[:, :, -1][:, :, None, None] * jnp.eye(width, dtype=jnp.float32) - jnp.einsum(
        "hcte,hctf->hcef", keys_tail, wy_key, precision=highest
    )
    offset = jnp.einsum("hcte,hctf->hcef", keys_tail, wy_value, precision=highest)
    local_out = jnp.einsum("hcts,hcsf->hctf", mixing, wy_value, precision=highest)
    entry_map = growth[:, :, :, None] * queries - jnp.einsum(
        "hcts,hcse->hcte", mixing, wy_key, precision=highest
    )
    return (transfer, offset, local_out, entry_map)


def advance(carried, terms):
    return (compose(carried, terms), carried)


def body(
    layer_in,
    attn_gain,
    qkv_weight,
    log_decay,
    write_rate,
    head_gain,
    out_weight,
    ffn_gain,
    gate_weight,
    up_weight,
    down_weight,
):
    length = layer_in.shape[0]
    slice_width = layer_in.shape[1]
    full_width = ffn_gain.shape[0]
    width = head_gain.shape[0]
    local_heads = qkv_weight.shape[2] // width
    span = min(64, length)
    pieces = length // span
    whole_rows = lax.all_gather(layer_in, "tp", axis=1, tiled=True).astype(jnp.float32)
    normed = (
        whole_rows
        * lax.rsqrt(jnp.mean(whole_rows * whole_rows, axis=1, keepdims=True) + norm_floor)
        * attn_gain
    ).astype(jnp.bfloat16)
    projected = jnp.einsum("ld,cde->cle", normed, qkv_weight, preferred_element_type=jnp.float32)
    projected = projected.reshape(3, length, local_heads, width).transpose(0, 2, 1, 3)
    projected = projected.reshape(3, local_heads, pieces, span, width)
    queries = unit_rows(projected[0])
    key_rows = unit_rows(projected[1])
    values = projected[2]
    transfer, offset, local_out, entry_map = block_terms(
        queries,
        key_rows,
        values,
        log_decay.reshape(local_heads, pieces, span),
        write_rate.reshape(local_heads, pieces, span),
    )
    start = (
        jnp.broadcast_to(jnp.eye(width, dtype=jnp.float32), (local_heads, width, width)),
        jnp.zeros((local_heads, width, width), jnp.float32),
    )
    device_terms, before = lax.scan(
        advance, start, (transfer.transpose(1, 0, 2, 3), offset.transpose(1, 0, 2, 3))
    )
    local_out = local_out + jnp.einsum("hcte,chef->hctf", entry_map, before[1], precision=highest)
    entry_map = jnp.einsum("hcte,chef->hctf", entry_map, before[0], precision=highest)
    local_out = local_out.reshape(local_heads, length, width)
    entry_map = entry_map.reshape(local_heads, length, width)
    prefix = prefix_by_axis(device_terms, SEQ, compose, start)
    heads_raw = local_out + jnp.einsum("hte,hef->htf", entry_map, prefix[1], precision=highest)
    heads_out = (
        heads_raw
        * lax.rsqrt(jnp.mean(heads_raw * heads_raw, axis=-1, keepdims=True) + head_floor)
        * head_gain
    )
    heads_out = (
        heads_out.transpose(1, 0, 2).reshape(length, local_heads * width).astype(jnp.bfloat16)
    )
    attn_terms = jnp.dot(heads_out, out_weight, preferred_element_type=jnp.float32)
    attn_slice = summed_on_arrival(attn_terms.astype(jnp.bfloat16), "tp", 1)
    residual = layer_in.astype(jnp.float32) + attn_slice
    squares = of_everyone(jnp.sum(residual * residual, axis=1), "tp")
    gain_slice = lax.dynamic_slice_in_dim(ffn_gain, lax.axis_index("tp") * slice_width, slice_width)
    normed_part = (
        residual * lax.rsqrt(squares / full_width + norm_floor)[:, None] * gain_slice
    ).astype(jnp.bfloat16)
    normed_mid = lax.all_gather(normed_part, "tp", axis=1, tiled=True)
    gate_act = jnp.dot(normed_mid, gate_weight, preferred_element_type=jnp.float32)
    up_act = jnp.dot(normed_mid, up_weight, preferred_element_type=jnp.float32)
    hidden = (jax.nn.silu(gate_act) * up_act).astype(jnp.bfloat16)
    ffn_terms = jnp.dot(hidden, down_weight, preferred_element_type=jnp.float32)
    ffn_slice = summed_on_arrival(ffn_terms.astype(jnp.bfloat16), "tp", 1)
    return (residual + ffn_slice).astype(jnp.bfloat16)


def solution(mesh):
    torus = Mesh(mesh.devices.reshape(4, 8, 2, mesh.shape["tp"]), ("seq_0", "seq_1", "seq_2", "tp"))
    in_specs = (
        P(SEQ, "tp"),
        P(),
        P(None, None, "tp"),
        P("tp", SEQ),
        P("tp", SEQ),
        P(),
        P("tp", None),
        P(),
        P(None, "tp"),
        P(None, "tp"),
        P("tp", None),
    )
    out_specs = P(SEQ, "tp")
    return jax.shard_map(body, mesh=torus, in_specs=in_specs, out_specs=out_specs, check_vma=False)
```

profile of v0, /device:TPU:2, one launch (start us, length us, event | category | flops | bytes accessed | tf_op | source)
XLA Modules:
  0.0 475.5 jit_solution(16160280800578878604)
XLA Ops:
  10.0 44.2 %all-gather.9.cloned.1.call-done = bf16[768,2048]{1,0:T(8,128)(2,1)} async-done(((bf16[768,512]{1,0:T(8,128)(2,1)}), bf16[768,2048]{1,0:T(8,128)(2,1)}) %all-gather.9.cloned.1.call-update) | async-done | bytes 3145744 | tf_op jit(solution)/shard_map/all_gather | solution.py:136
  54.2 2.7 fusion.11
  57.0 3.1 fusion.15
  62.5 1.4 multiply_multiply_fusion
  63.8 1.8 fusion.28
  65.6 119.1 %custom-call.4 = f32[2,12,1,64,64]{3,4,2,1,0:T(8,128)} custom-call(f32[2,12,1,64,64]{4,3,2,1,0:T(8,128)S(1)} %fusion.28), custom_call_target="InvertDiagBlocksLowerTriangular" | custom-call | tf_op jit(solution)/shard_map/jit(_solve_triangular)/vmap(vmap())/triangular_solve | solution.py:96
  184.7 1.6 convolution_multiply_fusion.1
  186.4 1.6 fusion.19
  188.0 1.8 fusion.35
  190.9 4.3 convolution_bitcast_fusion
  195.1 3.2 bitcast_subtract_fusion
  198.4 27.1 %while.17 = (s32[]{:T(128)}, f32[2,128,128]{2,1,0:T(8,128)S(1)}, f32[2,128,128]{2,1,0:T(8,128)S(1)}, f32[12,2,128,128]{3,2,0,1:T(8,128)}, f32[12,2,128,128]{3,2,...) while((s32[]{:T(128)}, f32[2,128,128]{2,1,0:T(8,128)S(1)}, ...), condition=%wide.region_5.6_spmd.clone, body=%wide.region_4.5_spmd.clone.sunk | while | flops 100761600 | bytes 1967735 | solution.py:159
  199.4 1.2 convolution_add_fusion.19
  201.7 1.2 convolution_add_fusion.19
  203.9 1.2 convolution_add_fusion.19
  225.5 3.1 convolution_add_fusion.2
  228.9 2.9 fusion.120
  231.8 1.9 all-gather
  234.1 27.0 %all-gather.1 = bf16[16,128,128]{2,1,0:T(8,128)(2,1)S(1)} all-gather(bf16[2,128,128]{2,1,0:T(8,128)(2,1)S(1)} %get-tuple-element.132), channel_id=3, replica_groups=mesh['seq_0'=4,'seq_1'=8,'seq_2'=2,'tp'=4] {'seq_1'}, dimensions={0}, use_global_device_ids=true | all-gather | bytes 589824 | tf_op jit(solution)/shard_map/all_gather | solution.py:25
  262.9 12.2 %all-gather.2 = bf16[8,128,128]{2,1,0:T(8,128)(2,1)S(1)} all-gather(bf16[2,128,128]{2,1,0:T(8,128)(2,1)S(1)} %get-tuple-element.134), channel_id=4, replica_groups=mesh['seq_0'=4,'seq_1'=8,'seq_2'=2,'tp'=4] {'seq_0'}, dimensions={0}, use_global_device_ids=true | all-gather | bytes 327680 | tf_op jit(solution)/shard_map/all_gather | solution.py:25
  275.2 1.9 all-gather.3
  277.5 25.4 %all-gather.4 = bf16[16,128,128]{2,1,0:T(8,128)(2,1)S(1)} all-gather(bf16[2,128,128]{2,1,0:T(8,128)(2,1)S(1)} %get-tuple-element.136), channel_id=6, replica_groups=mesh['seq_0'=4,'seq_1'=8,'seq_2'=2,'tp'=4] {'seq_1'}, dimensions={0}, use_global_device_ids=true | all-gather | bytes 589824 | tf_op jit(solution)/shard_map/all_gather | solution.py:25
  304.6 12.2 %all-gather.5 = bf16[8,128,128]{2,1,0:T(8,128)(2,1)S(1)} all-gather(bf16[2,128,128]{2,1,0:T(8,128)(2,1)S(1)} %get-tuple-element.138), channel_id=7, replica_groups=mesh['seq_0'=4,'seq_1'=8,'seq_2'=2,'tp'=4] {'seq_0'}, dimensions={0}, use_global_device_ids=true | all-gather | bytes 327680 | tf_op jit(solution)/shard_map/all_gather | solution.py:25
  321.7 32.0 %all_to_all.16 = bf16[4,768,512]{2,1,0:T(8,128)(2,1)S(1)} all-to-all(bf16[4,768,512]{2,1,0:T(8,128)(2,1)S(1)} %bitcast.139), channel_id=1, replica_groups=mesh['seq_0'=4,'seq_1'=8,'seq_2'=2,'tp'=4] {'tp'}, dimensions={0} | all-to-all | bytes 6291456 | tf_op jit(solution)/shard_map/all_to_all | solution.py:47
  356.1 3.3 all-to-all-start.1
  360.3 4.3 all-to-all-done.1
  365.8 39.8 %all-gather.11.cloned.1.call-done = bf16[768,2048]{1,0:T(8,128)(2,1)} async-done(((bf16[768,512]{1,0:T(8,128)(2,1)}), bf16[768,2048]{1,0:T(8,128)(2,1)}) %all-gather.11.cloned.1.call-update) | async-done | bytes 3145744 | tf_op jit(solution)/shard_map/all_gather | solution.py:184
  405.6 6.7 %fusion.122 = f32[768,640]{1,0:T(8,128)} fusion(bf16[768,2048]{1,0:T(8,128)(2,1)} %all-gather.11.cloned.1.call-done, bf16[2048,640]{1,0:T(8,128)(2,1)} %param.21), kind=kOutput, calls=%fused_computation.182 | convolution fusion | flops 2013265920 | bytes 7733248 | tf_op jit(solution)/shard_map/dot_general | solution.py:185
  412.4 10.6 %convolution_convert_fusion = bf16[768,2048]{1,0:T(8,128)(2,1)} fusion(bf16[640,2048]{1,0:T(8,128)(2,1)} %param.23, f32[768,640]{1,0:T(8,128)} %fusion.122, bf16[768,2048]{1,0:T(8,128)(2,1)S(1)} %copy-done.12, bf16[2048,640]{1,0:T(8,128)(2,1)} %param.22), kind=kOutput, calls=%fused_computation.21 | convolution fusion | flops 4031053824 | bytes 13500416 | tf_op jit(solution)/shard_map/dot_general | solution.py:188
  422.9 2.2 copy.95
  425.1 40.4 %all_to_all.17 = bf16[4,768,512]{2,1,0:T(8,128)(2,1)S(1)} all-to-all(bf16[4,768,512]{2,1,0:T(8,128)(2,1)S(1)} %bitcast.140), channel_id=1, replica_groups=mesh['seq_0'=4,'seq_1'=8,'seq_2'=2,'tp'=4] {'tp'}, dimensions={0} | all-to-all | bytes 6291456 | tf_op jit(solution)/shard_map/all_to_all | solution.py:47
  467.1 1.4 add_convert_fusion
  (159 shorter events, 45.0 us)
Async XLA Ops:
  6.5 50.4 %copy-start = (bf16[3,2048,256]{2,1,0:T(8,128)(2,1)S(1)}, bf16[3,2048,256]{2,1,0:T(8,128)(2,1)}, u32[]{:S(2)}) copy-start(bf16[3,2048,256]{2,1,0:T(8,128)(2,1)} %param.15) | copy-start | bytes 9437188
  6.5 47.7 %all-gather.9.cloned.1.call-start = ((), (), s32[]{:S(2)}) async-start(), calls=%async_computation.3 | async-start | bytes 3932160 | tf_op jit(solution)/shard_map/all_gather | solution.py:136
  7.3 49.7 %copy-start.13 = (f32[2048]{0:T(1024)S(1)}, f32[2048]{0:T(1024)}, u32[]{:S(2)}) copy-start(f32[2048]{0:T(1024)} %param.14) | copy-start | bytes 24580
  54.2 2.8 copy-start.6
  65.6 120.8 %copy-start.7 = (f32[2,12,64,128]{3,2,1,0:T(8,128)S(1)}, f32[2,12,64,128]{3,2,1,0:T(8,128)}, u32[]{:S(2)}) copy-start(f32[2,12,64,128]{3,2,1,0:T(8,128)} %broadcast_multiply_fusion) | copy-start | bytes 2359300
  184.7 1.7 copy-start.8
  184.7 1.7 copy-start.10
  318.6 1.5 copy-start.11
  319.2 1.2 copy-start.9
  353.7 1.1 copy-start.4
  354.9 10.9 %copy-start.2 = (f32[768,512]{1,0:T(8,128)}, f32[768,512]{1,0:T(8,128)S(1)}, u32[]{:S(2)}) copy-start(f32[768,512]{1,0:T(8,128)S(1)} %convert_reduce_fusion.1) | copy-start | bytes 4718596
  356.1 8.6 %all-to-all-start.1 = ((f32[4,1,768]{2,1,0:T(1,128)}), f32[4,1,768]{2,1,0:T(1,128)S(1)}, u32[]{:S(2)}, u32[]{:S(2)}) async-start(f32[4,1,768]{2,1,0:T(1,128)} %broadcast_in_dim.60), calls=%async_computation.1 | async-start | bytes 24576 | tf_op jit(solution)/shard_map/all_to_all | solution.py:53
  359.3 46.3 %all-gather.11.cloned.1.call-start = ((), (), s32[]{:S(2)}) async-start(), calls=%async_computation.4 | async-start | bytes 3932160 | tf_op jit(solution)/shard_map/all_gather | solution.py:184
  405.6 6.7 %copy-start.12 = (bf16[768,2048]{1,0:T(8,128)(2,1)S(1)}, bf16[768,2048]{1,0:T(8,128)(2,1)}, u32[]{:S(2)}) copy-start(bf16[768,2048]{1,0:T(8,128)(2,1)} %all-gather.11.cloned.1.call-done) | copy-start | bytes 9437188
  465.5 1.4 copy-start.3
  465.5 1.6 copy-start.5
  465.5 3.0 copy-start.1
Sparse Core Ops, SparseCore 0:
  9.1 45.0 all-gather.8
  365.9 39.6 all-gather.10
where the time goes:
time: 482 us; the launch traced here: 476 us
  blocking collectives  153 us (32%)
  other arithmetic  138 us (29%)
  waiting for transfers between devices  89 us (18%)
  matrix products  67.4 us (14%)
  between operations  14.3 us (3%)
  local copies, waits for them, and re-layouts  9.61 us (2%)
    another operation x3, other arithmetic, block_terms(): jax.scipy.linalg.solve_triangular(system, right_side, lower=True, unit_di...  119 us
    all_gather x6, blocking collectives, prefix_by_axis(): lax.all_gather(part.astype(kind), axis)  80.7 us
    all_to_all x2, blocking collectives, summed_on_arrival(): lax.all_to_all(in_blocks(shard, dim, peers), axis, 0, 0, tiled=True)  72.4 us
    all_gather x1, waiting for transfers between devices, body(): lax.all_gather(layer_in, 'tp', axis=1, tiled=True).astype(jnp.float32)  44.2 us
    all_gather x1, waiting for transfers between devices, body(): normed_mid = lax.all_gather(normed_part, 'tp', axis=1, tiled=True)  39.8 us
    dot_general x29, matrix products, compose(): jnp.einsum('hij,hjk->hik', second_map, first_shift, precision=highest)  17.9 us
    dot_general x1, matrix products, body(): ffn_terms = jnp.dot(hidden, down_weight, preferred_element_type=jnp.float32)  10.6 us
  transfers between devices with their start and end apart: 3, of which 3 were waited for; matrix products, arithmetic and copies ran while one was open for 1% of the time, Pallas kernels for 0%

commit v1 on v0

--- a/solution.py
+++ b/solution.py
@@ -181,7 +181,26 @@
     normed_part = (
         residual * lax.rsqrt(squares / full_width + norm_floor)[:, None] * gain_slice
     ).astype(jnp.bfloat16)
-    normed_mid = lax.all_gather(normed_part, "tp", axis=1, tiled=True)
+    size, index, span_2 = (lax.axis_size("tp"), lax.axis_index("tp"), normed_part.shape[1])
+    right = [(i, (i + 1) % size) for i in range(size)]
+    left = [(i, (i - 1) % size) for i in range(size)]
+    out = jnp.zeros(
+        (*normed_part.shape[:1], size * span_2, *normed_part.shape[1 + 1 :]), normed_part.dtype
+    )
+    out = lax.dynamic_update_slice_in_dim(out, normed_part, index * span_2, axis=1)
+    from_left = from_right = normed_part
+    halfway = size // 2
+    for step in range(1, halfway + 1):
+        from_left = lax.ppermute(from_left, "tp", right)
+        out = lax.dynamic_update_slice_in_dim(
+            out, from_left, (index - step) % size * span_2, axis=1
+        )
+        if step < size - halfway:
+            from_right = lax.ppermute(from_right, "tp", left)
+            out = lax.dynamic_update_slice_in_dim(
+                out, from_right, (index + step) % size * span_2, axis=1
+            )
+    normed_mid = out
     gate_act = jnp.dot(normed_mid, gate_weight, preferred_element_type=jnp.float32)
     up_act = jnp.dot(normed_mid, up_weight, preferred_element_type=jnp.float32)
     hidden = (jax.nn.silu(gate_act) * up_act).astype(jnp.bfloat16)

time: 482 us -> 460 us (0.954)
  blocking collectives: 153 us -> 133 us
  waiting for transfers between devices: 89 us -> 70.7 us
  matrix products: 67.4 us -> 77.2 us
    all_gather x1 -> x0, waiting for transfers between devices: 39.8 us -> none  [body(): normed_mid = lax.all_gather(normed_part, 'tp', axis=1, tiled=True)]
    ppermute x0 -> x3, waiting for transfers between devices: none -> 21.2 us  [the longest x2 21.2 us: body(): from_left = lax.ppermute(from_left, 'tp', right)]
    all_to_all x2, blocking collectives: 72.4 us -> 52.3 us  [summed_on_arrival(): lax.all_to_all(in_blocks(shard, dim, peers), axis, 0, 0, tiled=True)]
    dot_general x24, matrix products: 5.83 us -> 16.9 us  [compose(): jnp.einsum('hij,hjk->hik', second_map, first_map, precision=highest)]
  transfers between devices with their start and end apart: 3 -> 5, of which waited for: 3 -> 4; matrix products, arithmetic and copies ran while one was open for 1% -> 1% of each run, Pallas kernels for 0% -> 0%
where the time goes in v1:
time: 460 us; the launch traced here: 454 us
  other arithmetic  137 us (30%)
  blocking collectives  133 us (29%)
  matrix products  77.2 us (17%)
  waiting for transfers between devices  70.7 us (15%)
  between operations  14.3 us (3%)
  local copies, waits for them, and re-layouts  13.9 us (3%)
  starting transfers between devices  6.69 us (1%)
    another operation x3, other arithmetic, block_terms(): jax.scipy.linalg.solve_triangular(system, right_side, lower=True, unit_di...  119 us
    all_gather x6, blocking collectives, prefix_by_axis(): lax.all_gather(part.astype(kind), axis)  80.8 us
    all_to_all x2, blocking collectives, summed_on_arrival(): lax.all_to_all(in_blocks(shard, dim, peers), axis, 0, 0, tiled=True)  52.3 us
    all_gather x1, waiting for transfers between devices, body(): lax.all_gather(layer_in, 'tp', axis=1, tiled=True).astype(jnp.float32)  44.2 us
    ppermute x2, waiting for transfers between devices, body(): from_left = lax.ppermute(from_left, 'tp', right)  21.2 us
    dot_general x29, matrix products, compose(): jnp.einsum('hij,hjk->hik', second_map, first_shift, precision=highest)  18.5 us
    dot_general x24, matrix products, compose(): jnp.einsum('hij,hjk->hik', second_map, first_map, precision=highest)  16.9 us
    dot_general x1, matrix products, body(): ffn_terms = jnp.dot(hidden, down_weight, preferred_element_type=jnp.float32)  9.78 us
  transfers between devices with their start and end apart: 5, of which 4 were waited for; matrix products, arithmetic and copies ran while one was open for 1% of the time, Pallas kernels for 0%

profile of v1, /device:TPU:2, one launch (start us, length us, event | category | flops | bytes accessed | tf_op | source)
XLA Modules:
  0.0 453.8 jit_solution(14835362353736123167)
XLA Ops:
  10.0 44.2 %all-gather.8.cloned.1.call-done = bf16[768,2048]{1,0:T(8,128)(2,1)} async-done(((bf16[768,512]{1,0:T(8,128)(2,1)}), bf16[768,2048]{1,0:T(8,128)(2,1)}) %all-gather.8.cloned.1.call-update) | async-done | bytes 3145744 | tf_op jit(solution)/shard_map/all_gather | solution.py:136
  54.2 2.7 fusion.11
  57.0 3.1 fusion.15
  61.3 1.8 fusion.28
  63.1 119.1 %custom-call.4 = f32[2,12,1,64,64]{3,4,2,1,0:T(8,128)} custom-call(f32[2,12,1,64,64]{4,3,2,1,0:T(8,128)S(1)} %fusion.28), custom_call_target="InvertDiagBlocksLowerTriangular" | custom-call | tf_op jit(solution)/shard_map/jit(_solve_triangular)/vmap(vmap())/triangular_solve | solution.py:96
  182.2 1.4 multiply_multiply_fusion
  183.8 1.7 convolution_multiply_fusion.1
  185.5 1.6 fusion.19
  189.1 4.3 convolution_bitcast_fusion
  193.4 4.4 bitcast_subtract_fusion
  197.8 39.0 %while.17 = (s32[]{:T(128)}, f32[2,128,128]{2,1,0:T(8,128)S(1)}, f32[2,128,128]{2,1,0:T(8,128)S(1)}, f32[12,2,128,128]{3,2,0,1:T(8,128)}, f32[12,2,128,128]{3,2,...) while((s32[]{:T(128)}, f32[2,128,128]{2,1,0:T(8,128)S(1)}, ...), condition=%wide.region_5.6_spmd.clone, body=%wide.region_4.5_spmd.clone.sunk | while | flops 100761600 | bytes 1967735 | solution.py:159
  198.6 1.2 convolution_add_fusion.19
  236.8 3.0 fusion.123
  239.8 2.5 convolution_add_fusion.2
  242.3 1.4 copy.68
  243.7 1.9 all-gather
  245.6 1.9 all-gather.3
  248.4 27.0 %all-gather.1 = bf16[16,128,128]{2,1,0:T(8,128)(2,1)S(1)} all-gather(bf16[2,128,128]{2,1,0:T(8,128)(2,1)S(1)} %get-tuple-element.134), channel_id=3, replica_groups=mesh['seq_0'=4,'seq_1'=8,'seq_2'=2,'tp'=4] {'seq_1'}, dimensions={0}, use_global_device_ids=true | all-gather | bytes 589824 | tf_op jit(solution)/shard_map/all_gather | solution.py:25
  277.2 12.2 %all-gather.2 = bf16[8,128,128]{2,1,0:T(8,128)(2,1)S(1)} all-gather(bf16[2,128,128]{2,1,0:T(8,128)(2,1)S(1)} %get-tuple-element.136), channel_id=4, replica_groups=mesh['seq_0'=4,'seq_1'=8,'seq_2'=2,'tp'=4] {'seq_0'}, dimensions={0}, use_global_device_ids=true | all-gather | bytes 327680 | tf_op jit(solution)/shard_map/all_gather | solution.py:25
  289.4 25.3 %all-gather.4 = bf16[16,128,128]{2,1,0:T(8,128)(2,1)S(1)} all-gather(bf16[2,128,128]{2,1,0:T(8,128)(2,1)S(1)} %get-tuple-element.138), channel_id=6, replica_groups=mesh['seq_0'=4,'seq_1'=8,'seq_2'=2,'tp'=4] {'seq_1'}, dimensions={0}, use_global_device_ids=true | all-gather | bytes 589824 | tf_op jit(solution)/shard_map/all_gather | solution.py:25
  317.4 12.4 %all-gather.5 = bf16[8,128,128]{2,1,0:T(8,128)(2,1)S(1)} all-gather(bf16[2,128,128]{2,1,0:T(8,128)(2,1)S(1)} %get-tuple-element.140), channel_id=7, replica_groups=mesh['seq_0'=4,'seq_1'=8,'seq_2'=2,'tp'=4] {'seq_0'}, dimensions={0}, use_global_device_ids=true | all-gather | bytes 327680 | tf_op jit(solution)/shard_map/all_gather | solution.py:25
  333.8 27.6 %all_to_all.16 = bf16[4,768,512]{2,1,0:T(8,128)(2,1)S(1)} all-to-all(bf16[4,768,512]{2,1,0:T(8,128)(2,1)S(1)} %bitcast.139), channel_id=1, replica_groups=mesh['seq_0'=4,'seq_1'=8,'seq_2'=2,'tp'=4] {'tp'}, dimensions={0} | all-to-all | bytes 6291456 | tf_op jit(solution)/shard_map/all_to_all | solution.py:47
  363.7 3.3 all-to-all-start.1
  367.7 4.6 %all-to-all-done.1 = f32[4,1,768]{2,1,0:T(1,128)S(1)} async-done(((f32[4,1,768]{2,1,0:T(1,128)}), f32[4,1,768]{2,1,0:T(1,128)S(1)}, u32[]{:S(2)}, u32[]{:S(2)}) %all-to-all-start.1) | async-done | bytes 12320 | tf_op jit(solution)/shard_map/all_to_all | solution.py:53
  372.4 2.0 broadcast_in_dim.63
  376.3 2.7 collective-permute-start.1
  379.0 10.0 %collective-permute-done = bf16[768,512]{1,0:T(8,128)(2,1)S(1)} collective-permute-done((bf16[768,512]{1,0:T(8,128)(2,1)S(1)}, bf16[768,512]{1,0:T(8,128)(2,1)S(1)}, u32[]{:S(2)}, u32[]{:S(2)}) %collective-permute-start) | collective-permute-done | bytes 786464 | tf_op jit(solution)/shard_map/ppermute | solution.py:194
  391.0 11.2 %collective-permute-done.2 = bf16[768,512]{1,0:T(8,128)(2,1)S(1)} collective-permute-done((bf16[768,512]{1,0:T(8,128)(2,1)S(1)}, bf16[768,512]{1,0:T(8,128)(2,1)S(1)}, u32[]{:S(2)}, u32[]{:S(2)}) %collective-permute-start.2) | collective-permute-done | bytes 786464 | tf_op jit(solution)/shard_map/ppermute | solution.py:194
  403.2 5.8 %fusion.125 = f32[768,640]{1,0:T(8,128)} fusion(bf16[768,2048]{1,0:T(8,128)(2,1)} %constant_dynamic-update-slice_fusion, bf16[2048,640]{1,0:T(8,128)(2,1)S(1)} %copy-done.12), kind=kOutput, calls=%fused_computation.188 | convolution fusion | flops 2013265920 | bytes 7733248 | tf_op jit(solution)/shard_map/dot_general | solution.py:204
  409.1 9.8 %convolution_convert_fusion = bf16[768,2048]{1,0:T(8,128)(2,1)S(1)} fusion(bf16[640,2048]{1,0:T(8,128)(2,1)} %param.23, f32[768,640]{1,0:T(8,128)} %fusion.125, bf16[768,2048]{1,0:T(8,128)(2,1)} %constant_dynamic-update-slice_fusion, bf16[2048,640]{1,0:T(8,128)(2,1)} %param.22), kind=kOutput, calls=%fused_computation.21 | convolution fusion | flops 4031053824 | bytes 13500416 | tf_op jit(solution)/shard_map/dot_general | solution.py:207
  419.2 24.6 %all_to_all.17 = bf16[4,768,512]{2,1,0:T(8,128)(2,1)S(1)} all-to-all(bf16[4,768,512]{2,1,0:T(8,128)(2,1)S(1)} %bitcast.140), channel_id=1, replica_groups=mesh['seq_0'=4,'seq_1'=8,'seq_2'=2,'tp'=4] {'tp'}, dimensions={0} | all-to-all | bytes 6291456 | tf_op jit(solution)/shard_map/all_to_all | solution.py:47
  445.4 1.4 add_convert_fusion
  (166 shorter events, 62.7 us)
Async XLA Ops:
  6.5 50.4 %copy-start = (bf16[3,2048,256]{2,1,0:T(8,128)(2,1)S(1)}, bf16[3,2048,256]{2,1,0:T(8,128)(2,1)}, u32[]{:S(2)}) copy-start(bf16[3,2048,256]{2,1,0:T(8,128)(2,1)} %param.15) | copy-start | bytes 9437188
  6.5 47.7 %all-gather.8.cloned.1.call-start = ((), (), s32[]{:S(2)}) async-start(), calls=%async_computation.3 | async-start | bytes 3932160 | tf_op jit(solution)/shard_map/all_gather | solution.py:136
  7.3 49.7 %copy-start.13 = (f32[2048]{0:T(1024)S(1)}, f32[2048]{0:T(1024)}, u32[]{:S(2)}) copy-start(f32[2048]{0:T(1024)} %param.14) | copy-start | bytes 24580
  54.2 2.8 copy-start.6
  183.8 1.7 copy-start.7
  183.8 1.7 copy-start.10
  236.8 3.0 copy-start.8
  330.7 1.5 copy-start.11
  331.2 1.2 copy-start.9
  361.4 1.1 copy-start.4
  362.5 11.9 %copy-start.2 = (f32[768,512]{1,0:T(8,128)}, f32[768,512]{1,0:T(8,128)S(1)}, u32[]{:S(2)}) copy-start(f32[768,512]{1,0:T(8,128)S(1)} %convert_reduce_fusion.1) | copy-start | bytes 4718596
  363.7 8.6 %all-to-all-start.1 = ((f32[4,1,768]{2,1,0:T(1,128)}), f32[4,1,768]{2,1,0:T(1,128)S(1)}, u32[]{:S(2)}, u32[]{:S(2)}) async-start(f32[4,1,768]{2,1,0:T(1,128)} %broadcast_in_dim.64), calls=%async_computation.1 | async-start | bytes 24576 | tf_op jit(solution)/shard_map/all_to_all | solution.py:53
  375.6 13.4 %collective-permute-start = (bf16[768,512]{1,0:T(8,128)(2,1)S(1)}, bf16[768,512]{1,0:T(8,128)(2,1)S(1)}, u32[]{:S(2)}, u32[]{:S(2)}) collective-permute-start(bf16[768,512]{1,0:T(8,128)(2,1)S(1)} %get-tuple-element.125), channel_id=1, source_target_pairs={{0,1},{1,2},{2,3},{3,0},{4,5},{5,6},{6,7},{7,4},{8,9},{9,10},{10,1... | collective-permute-start | bytes 2359304 | tf_op jit(solution)/shard_map/ppermute | solution.py:194
  376.3 13.7 %collective-permute-start.1 = (bf16[768,512]{1,0:T(8,128)(2,1)S(1)}, bf16[768,512]{1,0:T(8,128)(2,1)S(1)}, u32[]{:S(2)}, u32[]{:S(2)}) collective-permute-start(bf16[768,512]{1,0:T(8,128)(2,1)S(1)} %get-tuple-element.125), channel_id=1, source_target_pairs={{0,3},{1,0},{2,1},{3,2},{4,7},{5,4},{6,5},{7,6},{8,11},{9,8},{10,9... | collective-permute-start | bytes 2359304 | tf_op jit(solution)/shard_map/ppermute | solution.py:199
  389.0 13.2 %collective-permute-start.2 = (bf16[768,512]{1,0:T(8,128)(2,1)S(1)}, bf16[768,512]{1,0:T(8,128)(2,1)S(1)}, u32[]{:S(2)}, u32[]{:S(2)}) collective-permute-start(bf16[768,512]{1,0:T(8,128)(2,1)S(1)} %collective-permute-done), channel_id=1, source_target_pairs={{0,1},{1,2},{2,3},{3,0},{4,5},{5,6},{6,7},{7,4},{8,9},{9,10},{10,1... | collective-permute-start | bytes 2359304 | tf_op jit(solution)/shard_map/ppermute | solution.py:194
  390.0 13.3 %copy-start.12 = (bf16[2048,640]{1,0:T(8,128)(2,1)S(1)}, bf16[2048,640]{1,0:T(8,128)(2,1)}, u32[]{:S(2)}) copy-start(bf16[2048,640]{1,0:T(8,128)(2,1)} %param.21) | copy-start | bytes 7864324
  443.8 1.4 copy-start.3
  443.8 1.6 copy-start.5
  443.8 3.0 copy-start.1
Sparse Core Ops, SparseCore 0:
  9.1 45.0 all-gather.7
